TPU v7x, 256 devices: a whole 4x4x8 slice. The times are simulated.
256 devices in a mesh: owner: 16 (over z_lo, y), rows: 16 (over z_hi, x, core).
Axes of the slice: x: 4, y: 4, z: 8 (z_hi: 2, z_lo: 4; z = z_hi * 4 + z_lo), core: 2. Of those that a mesh axis runs over, the one named last changes fastest.
Arguments:
- master_down: float32 [16, 6400, 4096], P('owner', None, 'rows'), may hold values from -0.109375 to 0.109375
- router_weight: float32 [4096, 16], P('rows', 'owner'), may hold values from -0.09375 to 0.09375
- router_gain: float32 [4096], P('rows'), may hold values from 0.25 to 1.75
Outputs:
- final_down: bfloat16 [16, 6400, 4096], P('owner', 'rows')
- scale_down: float32 [16, 6400], P('owner', 'rows')
- serve_router: bfloat16 [4096, 16], replicated
All inputs are finite; a program needn't handle non-finite values. Where the computation divides by a largest or mean magnitude, that divisor is 1e-20 or more.
Results may differ from a plain program's by a relative error of at most 0.001.
Values may be sent and summed in bfloat16 or wider, within the bound.
A program may use at most 64 MiB of HBM per device.

v0:
```python
import jax
import jax.numpy as jnp
from jax import lax
from jax.sharding import PartitionSpec as P

D_MODEL = 4096


def sent_to_all(array, axis):
    length = lax.axis_size(axis)
    return lax.all_to_all(
        jnp.broadcast_to(array[None], (length, *array.shape)), axis, 0, 0, tiled=True
    )


def of_everyone(array, axis):
    return sent_to_all(array, axis).sum(axis=0)


def cut_along(array, dim, length):
    before, after = (array.shape[:dim], array.shape[dim + 1 :])
    return jnp.moveaxis(array.reshape(*before, length, -1, *after), dim, 0)


def edges_of(length, count):
    unit = 8 if length >= 8 * count else 1
    return [length // unit * k // count * unit for k in range(1, count)]


def laid_out(tiles, dim):
    dims = list(tiles.shape[1:])
    dims[dim] *= tiles.shape[0]
    return jnp.moveaxis(tiles, 0, dim).reshape(dims)


def several_exchanges(array, axis, pieces, split_dim, concat_dim):
    tiles = cut_along(array, split_dim, lax.axis_size(axis))
    widest = max(range(1, max(2, tiles.ndim - 1)), key=lambda d: tiles.shape[d])
    done = []
    for slab in jnp.split(tiles, edges_of(tiles.shape[widest], pieces), axis=widest):
        if slab.size:
            done.append(lax.all_to_all(slab, axis, split_axis=0, concat_axis=0, tiled=True))
    return laid_out(jnp.concatenate(done, axis=widest), concat_dim)


def gather_directly(array, axis, dim):
    tiles = sent_to_all(array, axis)
    return laid_out(tiles, dim)


def per_device(master_down, router_weight, router_gain):
    total_down = of_everyone(jnp.sum(jnp.abs(master_down), axis=2), "rows")
    scale_down = total_down / D_MODEL
    narrow_down = (master_down / jnp.expand_dims(scale_down, 2)).astype(jnp.bfloat16)
    final_down = several_exchanges(narrow_down, "rows", 2, 1, 2)
    scale_down = lax.dynamic_slice_in_dim(
        scale_down, lax.axis_index("rows") * final_down.shape[1], final_down.shape[1], axis=1
    )
    part_router = (router_weight * router_gain[:, None]).astype(jnp.bfloat16)
    row_router = gather_directly(part_router, "rows", 0)
    serve_router = gather_directly(row_router, "owner", 1)
    return (final_down, scale_down, serve_router)


def solution(mesh):
    return jax.shard_map(
        per_device,
        mesh=mesh,
        in_specs=(P("owner", None, "rows"), P("rows", "owner"), P("rows")),
        out_specs=(P("owner", "rows", None), P("owner", "rows"), P()),
        check_vma=False,
    )
```

profile of v0, /device:TPU:39, one launch (start us, length us, event | category | flops | bytes accessed | tf_op | source)
XLA Modules:
  0.0 156.9 jit_solution(938155393191317613)
XLA Ops:
  0.6 0.7 convert_reduce_fusion
  1.4 0.5 broadcast.22
  1.9 0.7 reduce.6
  2.6 0.6 reshape.45
  3.2 10.8 %all-to-all-start.3 = ((bf16[16,2,128]{2,1,0:T(2,128)(2,1)}), bf16[16,2,128]{2,1,0:T(2,128)(2,1)S(1)}, u32[]{:S(2)}, u32[]{:S(2)}) async-start(bf16[16,2,128]{2,1,0:T(2,128)(2,1)} %reshape.45), calls=%async_computation.3 | async-start | bytes 16384 | tf_op jit(solution)/shard_map/all_to_all | solution.py:11
  14.0 3.8 %abs_reduce_fusion = f32[6400]{0:T(1024)S(1)} fusion(f32[1,6400,256]{2,1,0:T(8,128)} %param.3), kind=kLoop, calls=%fused_computation.1 | loop fusion | flops 3270400 | bytes 6579200 | tf_op jit(solution)/shard_map/reduce_sum | solution.py:52
  17.8 3.9 %all-to-all-done.3 = bf16[16,2,128]{2,1,0:T(2,128)(2,1)S(1)} async-done(((bf16[16,2,128]{2,1,0:T(2,128)(2,1)}), bf16[16,2,128]{2,1,0:T(2,128)(2,1)S(1)}, u32[]{:S(2)}, u32[]{:S(2)}) %all-to-all-start.3) | async-done | bytes 8224 | tf_op jit(solution)/shard_map/all_to_all | solution.py:11
  21.7 1.0 broadcast_in_dim.12
  22.6 5.7 %all-to-all-start = ((f32[16,1,6400]{2,1,0:T(1,128)}), f32[16,1,6400]{2,1,0:T(1,128)S(1)}, u32[]{:S(2)}, u32[]{:S(2)}) async-start(f32[16,1,6400]{2,1,0:T(1,128)} %broadcast_in_dim.12), calls=%async_computation | async-start | bytes 819200 | tf_op jit(solution)/shard_map/all_to_all | solution.py:11
  28.6 1.4 reduce.7
  30.0 0.7 reshape.47
  30.8 13.5 %all-to-all-done = f32[16,1,6400]{2,1,0:T(1,128)S(1)} async-done(((f32[16,1,6400]{2,1,0:T(1,128)}), f32[16,1,6400]{2,1,0:T(1,128)S(1)}, u32[]{:S(2)}, u32[]{:S(2)}) %all-to-all-start) | async-done | bytes 409632 | tf_op jit(solution)/shard_map/all_to_all | solution.py:11
  44.3 5.8 %all-to-all-start.4 = ((bf16[16,2,2048]{2,1,0:T(2,128)(2,1)}), bf16[16,2,2048]{2,1,0:T(2,128)(2,1)S(1)}, u32[]{:S(2)}, u32[]{:S(2)}) async-start(bf16[16,2,2048]{2,1,0:T(2,128)(2,1)} %reshape.47), calls=%async_computation.4 | async-start | bytes 262144 | tf_op jit(solution)/shard_map/all_to_all | solution.py:11
  50.1 0.3 reduce_sum.19
  50.4 4.6 %divide_convert_fusion = bf16[1,6400,256]{2,1,0:T(8,128)(2,1)S(1)} fusion(f32[1,6400,256]{2,1,0:T(8,128)} %param.3, f32[6400]{0:T(1024)S(1)} %broadcast_multiply_fusion), kind=kLoop, calls=%fused_computation | loop fusion | flops 3276800 | bytes 9856000 | tf_op jit(solution)/shard_map/convert_element_type | solution.py:54
  55.1 1.4 fusion
  56.5 0.7 copy-done
  57.1 48.0 %all_to_all.25 = bf16[16,1,200,256]{3,2,1,0:T(8,128)(2,1)S(1)} all-to-all(bf16[16,1,200,256]{3,2,1,0:T(8,128)(2,1)S(1)} %get-tuple-element.3), channel_id=1, replica_groups=mesh['owner'=16,'rows'=16] {'rows'}, dimensions={0} | all-to-all | bytes 3276800 | tf_op jit(solution)/shard_map/all_to_all | solution.py:42
  105.1 5.5 %all-to-all-start.2 = ((bf16[16,1,200,256]{3,2,1,0:T(8,128)(2,1)}), bf16[16,1,200,256]{3,2,1,0:T(8,128)(2,1)S(1)}, u32[]{:S(2)}, u32[]{:S(2)}) async-start(bf16[16,1,200,256]{3,2,1,0:T(8,128)(2,1)} %get-tuple-element.4), calls=%async_computation.2 | async-start | bytes 3276800 | tf_op jit(solution)/shard_map/all_to_all | solution.py:42
  110.6 1.4 reshape.48
  112.0 0.8 copy.21
  112.8 1.3 dynamic-slice.3
  114.2 40.4 %all-to-all-done.2 = bf16[16,1,200,256]{3,2,1,0:T(8,128)(2,1)S(1)} async-done(((bf16[16,1,200,256]{3,2,1,0:T(8,128)(2,1)}), bf16[16,1,200,256]{3,2,1,0:T(8,128)(2,1)S(1)}, u32[]{:S(2)}, u32[]{:S(2)}) %all-to-all-start.2) | async-done | bytes 1638432 | tf_op jit(solution)/shard_map/all_to_all | solution.py:42
  154.8 2.1 %copy.18 = bf16[16,1,50,8,256]{4,3,0,2,1:T(8,128)(2,1)} copy(bf16[16,1,50,8,256]{4,3,2,1,0:T(8,128)(2,1)S(1)} %maximum_bitcast_fusion) | data formatting | bytes 6553600 | tf_op jit(solution)/shard_map/reshape | solution.py:33
  (11 shorter events, 0.6 us)
Async XLA Ops:
  3.2 18.5 %all-to-all-start.3 = ((bf16[16,2,128]{2,1,0:T(2,128)(2,1)}), bf16[16,2,128]{2,1,0:T(2,128)(2,1)S(1)}, u32[]{:S(2)}, u32[]{:S(2)}) async-start(bf16[16,2,128]{2,1,0:T(2,128)(2,1)} %reshape.45), calls=%async_computation.3 | async-start | bytes 16384 | tf_op jit(solution)/shard_map/all_to_all | solution.py:11
  22.6 21.7 %all-to-all-start = ((f32[16,1,6400]{2,1,0:T(1,128)}), f32[16,1,6400]{2,1,0:T(1,128)S(1)}, u32[]{:S(2)}, u32[]{:S(2)}) async-start(f32[16,1,6400]{2,1,0:T(1,128)} %broadcast_in_dim.12), calls=%async_computation | async-start | bytes 819200 | tf_op jit(solution)/shard_map/all_to_all | solution.py:11
  44.3 12.2 %all-to-all-start.4 = ((bf16[16,2,2048]{2,1,0:T(2,128)(2,1)}), bf16[16,2,2048]{2,1,0:T(2,128)(2,1)S(1)}, u32[]{:S(2)}, u32[]{:S(2)}) async-start(bf16[16,2,2048]{2,1,0:T(2,128)(2,1)} %reshape.47), calls=%async_computation.4 | async-start | bytes 262144 | tf_op jit(solution)/shard_map/all_to_all | solution.py:11
  50.4 4.6 %copy-start.1 = (f32[6400]{0:T(1024)}, f32[6400]{0:T(1024)S(1)}, u32[]{:S(2)}) copy-start(f32[6400]{0:T(1024)S(1)} %broadcast_multiply_fusion) | copy-start | bytes 76804
  56.5 0.7 copy-start
  105.1 49.5 %all-to-all-start.2 = ((bf16[16,1,200,256]{3,2,1,0:T(8,128)(2,1)}), bf16[16,1,200,256]{3,2,1,0:T(8,128)(2,1)S(1)}, u32[]{:S(2)}, u32[]{:S(2)}) async-start(bf16[16,1,200,256]{3,2,1,0:T(8,128)(2,1)} %get-tuple-element.4), calls=%async_computation.2 | async-start | bytes 3276800 | tf_op jit(solution)/shard_map/all_to_all | solution.py:42
where the time goes:
time: 157 us
  waiting for transfers between devices  57.9 us (37%)
  blocking collectives  48 us (31%)
  starting transfers between devices  27.9 us (18%)
  other arithmetic  11.7 us (7%)
  local copies, waits for them, and re-layouts  10.8 us (7%)
    all_to_all x1, blocking collectives, several_exchanges(): lax.all_to_all(slab, axis, split_axis=0, concat_axis=0, tiled=True)  48 us
    all_to_all x1, waiting for transfers between devices, several_exchanges(): lax.all_to_all(slab, axis, split_axis=0, concat_axis=0, tiled=True)  40.4 us
    all_to_all x3, starting transfers between devices, sent_to_all(): lax.all_to_all(jnp.broadcast_to(array[None], (length, *array.shape)), axi...  22.4 us
    all_to_all x3, waiting for transfers between devices, sent_to_all(): lax.all_to_all(jnp.broadcast_to(array[None], (length, *array.shape)), axi...  17.5 us
    all_to_all x1, starting transfers between devices, several_exchanges(): lax.all_to_all(slab, axis, split_axis=0, concat_axis=0, tiled=True)  5.53 us
    convert_element_type x1, other arithmetic, per_device(): (master_down / jnp.expand_dims(scale_down, 2)).astype(jnp.bfloat16)  4.63 us
    unnamed x12, local copies, waits for them, and re-layouts  4.11 us
    reduce_sum x1, other arithmetic, per_device(): total_down = of_everyone(jnp.sum(jnp.abs(master_down), axis=2), 'rows')  3.78 us
  transfers between devices with their start and end apart: 4, of which 3 were waited for; matrix products, arithmetic and copies ran while one was open for 10% of the time, Pallas kernels for 0%

commit v1 on v0

v1 whole, which is shorter than its diff:
```python
import functools

import jax
import jax.numpy as jnp
from jax import lax
from jax.experimental import pallas as pl
from jax.experimental.pallas import tpu as pltpu
from jax.sharding import PartitionSpec as P

MESH = pl.DeviceIdType.MESH
N = 16
ROWS = 400
COLS = 256
WIDTH = 4096
TILES = ROWS // 8

FAR = [(1, dx, dc) for dx in (0, 2, 1, 3) for dc in (0, 1)]
NEAR = [(0, dx, dc) for dx in (2, 1, 3) for dc in (0, 1)] + [(0, 0, 1)]
PEERS = FAR + NEAR
BACK = [PEERS.index((h, (4 - dx) % 4, dc)) for h, dx, dc in PEERS]
OWNERS = [(dz, dy) for dz in range(4) for dy in range(4)][1:]


def peer_row(me, step):
    half, dx, dc = step
    x = lax.rem(lax.rem(me // 2, 4) + dx, 4)
    return lax.rem(me // 8 + half, 2) * 8 + x * 2 + lax.rem(lax.rem(me, 2) + dc, 2)


def peer_owner(me, step):
    return lax.rem(me // 4 + step[0], 4) * 4 + lax.rem(lax.rem(me, 4) + step[1], 4)


def sums_of(block):
    part = jnp.sum(jnp.abs(block), axis=1, keepdims=True).reshape(TILES, 8, 1)
    shape = (TILES, 8, 128)
    place = lax.broadcasted_iota(jnp.int32, shape, 0) == lax.broadcasted_iota(jnp.int32, shape, 2)
    return jnp.sum(jnp.where(place, part, 0.0), axis=0)


def scaled(master, first, inverse, k):
    block = master[pl.ds(pl.multiple_of(first + 16 * k, 16), 16), :]
    by = jnp.concatenate(
        [jnp.broadcast_to(inverse[:, c : c + 1], (8, COLS)) for c in (2 * k, 2 * k + 1)], axis=0
    )
    return (block * by).astype(jnp.bfloat16)


def kernel(
    master_hbm, weight, gain, final, scale, router,
    master, narrow, sums, parts, totals, row, column,
    in_sem, part_s, part_r, total_s, total_r, tile_s, tile_r, row_s, row_r, pair_s, pair_r, half_s, half_r,
):
    me, owner = lax.axis_index("rows"), lax.axis_index("owner")
    rows_of = [peer_row(me, step) for step in PEERS]
    owners_of = [peer_owner(owner, step) for step in OWNERS]

    def send(src, dst, send_sem, recv_sem, to_owner, to_row):
        copy = pltpu.make_async_remote_copy(
            src_ref=src, dst_ref=dst, send_sem=send_sem, recv_sem=recv_sem,
            device_id=(to_owner, to_row), device_id_type=MESH,
        )
        copy.start()
        return copy

    def tile_at(device):
        return pl.ds(pl.multiple_of(device * ROWS, ROWS), ROWS)

    def columns_at(device):
        return pl.ds(pl.multiple_of(device * COLS, COLS), COLS)

    loads = []
    for d in range(N):
        load = pltpu.make_async_copy(
            master_hbm.at[0, pl.ds(d * ROWS, ROWS), :], master.at[pl.ds(d * ROWS, ROWS), :], in_sem.at[d]
        )
        load.start()
        loads.append(load)

    barrier = pltpu.get_barrier_semaphore()
    for r in rows_of:
        pl.semaphore_signal(barrier, inc=1, device_id=(owner, r), device_id_type=MESH)
    for o in owners_of:
        pl.semaphore_signal(barrier, inc=1, device_id=(o, me), device_id_type=MESH)

    row[...] = (weight[...] * gain[...])[None]
    for d in range(N):
        loads[d].wait()
        sums[d] = sums_of(master[pl.ds(d * ROWS, ROWS), :])
    pl.semaphore_wait(barrier, len(rows_of) + len(owners_of))

    waits = []
    part_copies = [
        send(sums.at[r], parts.at[me], part_s.at[i], part_r.at[i], owner, r) for i, r in enumerate(rows_of)
    ]
    row_copies = [
        send(row.at[0], column.at[owner], row_s.at[i], row_r.at[i], o, me) for i, o in enumerate(owners_of)
    ]
    parts[me] = sums[me]
    column[owner] = row[0]
    for copy in part_copies:
        copy.wait_recv()
    total = parts[0]
    for d in range(1, N):
        total = total + parts[d]
    totals[me] = total / WIDTH
    total_copies = [
        send(totals.at[me], totals.at[me], total_s.at[i], total_r.at[i], owner, r) for i, r in enumerate(rows_of)
    ]

    for copy in row_copies:
        copy.wait_recv()
    router[:, columns_at(me)] = jnp.concatenate([column[o] for o in range(N)], axis=0).astype(jnp.bfloat16)
    across = rows_of[0]

    mean = totals[me]
    shape = (128, 512)
    spread = (lax.broadcasted_iota(jnp.int32, shape, 1) // 8 == lax.broadcasted_iota(jnp.int32, shape, 0)).astype(jnp.float32)
    wide = jnp.dot(mean, spread, precision=lax.Precision.HIGHEST, preferred_element_type=jnp.float32)
    shape = (8, 512)
    keep = lax.rem(lax.broadcasted_iota(jnp.int32, shape, 1), 8) == lax.broadcasted_iota(jnp.int32, shape, 0)
    scale[...] = jnp.sum(jnp.where(keep, wide, 0.0), axis=0, keepdims=True)[:, :ROWS]

    pair = send(
        router.at[:, columns_at(me)], router.at[:, columns_at(me)], pair_s.at[0], pair_r.at[0], owner, across
    )

    def scale_tile(device, store):
        inverse = 1.0 / jnp.where(lax.broadcasted_iota(jnp.int32, (8, 128), 1) < TILES, totals[device], 1.0)
        for k in range(ROWS // 16):
            store(k, scaled(master, device * ROWS, inverse, k))

    def to_narrow(device):
        def store(k, value):
            narrow[pl.ds(pl.multiple_of(device * ROWS + 16 * k, 16), 16), :] = value

        return store

    tile_copies, half_copies = [], []
    for i, r in enumerate(rows_of):
        total_copies[BACK[i]].wait_recv()
        scale_tile(r, to_narrow(r))
        tile_copies.append(
            send(narrow.at[tile_at(r), :], final.at[:, columns_at(me)], tile_s.at[i], tile_r.at[i], owner, r)
        )
        if i == 1:
            pair.wait_recv()
            for j in range(len(NEAR)):
                for k, block in enumerate((me, across)):
                    half_copies.append(
                        send(
                            router.at[:, columns_at(block)], router.at[:, columns_at(block)],
                            half_s.at[j, k], half_r.at[j, k], owner, rows_of[len(FAR) + j],
                        )
                    )

    def to_final(k, value):
        final[16 * k : 16 * k + 16, columns_at(me)] = value

    scale_tile(me, to_final)
    for copy in part_copies + row_copies + total_copies + [pair]:
        copy.wait_send()
    for copy in half_copies + tile_copies:
        copy.wait()


def per_device(master_down, router_weight, router_gain):
    vmem = pl.BlockSpec(memory_space=pltpu.VMEM)
    dma = pltpu.SemaphoreType.DMA
    final, scale, router = pl.pallas_call(
        kernel,
        out_shape=(
            jax.ShapeDtypeStruct((ROWS, WIDTH), jnp.bfloat16),
            jax.ShapeDtypeStruct((1, ROWS), jnp.float32),
            jax.ShapeDtypeStruct((N, WIDTH), jnp.bfloat16),
        ),
        in_specs=[pl.BlockSpec(memory_space=pltpu.HBM), vmem, vmem],
        out_specs=(vmem, vmem, vmem),
        scratch_shapes=[
            pltpu.VMEM((N * ROWS, COLS), jnp.float32),
            pltpu.VMEM((N * ROWS, COLS), jnp.bfloat16),
            pltpu.VMEM((N, 8, 128), jnp.float32),
            pltpu.VMEM((N, 8, 128), jnp.float32),
            pltpu.VMEM((N, 8, 128), jnp.float32),
            pltpu.VMEM((1, 1, COLS), jnp.float32),
            pltpu.VMEM((N, 1, COLS), jnp.float32),
            dma((N,)),
            dma((len(PEERS),)), dma((len(PEERS),)),
            dma((len(PEERS),)), dma((len(PEERS),)),
            dma((len(PEERS),)), dma((len(PEERS),)),
            dma((len(OWNERS),)), dma((len(OWNERS),)),
            dma((1,)), dma((1,)),
            dma((len(NEAR), 2)), dma((len(NEAR), 2)),
        ],
        compiler_params=pltpu.CompilerParams(
            collective_id=0, has_side_effects=True, vmem_limit_bytes=48 << 20
        ),
    )(master_down, router_weight.reshape(1, COLS), router_gain.reshape(1, COLS))
    return final[None], scale, router.T


def solution(mesh):
    return jax.shard_map(
        per_device,
        mesh=mesh,
        in_specs=(P("owner", None, "rows"), P("rows", "owner"), P("rows")),
        out_specs=(P("owner", "rows", None), P("owner", "rows"), P()),
        check_vma=False,
    )
```

time: 157 us -> 103 us (0.66)
  the two profiles are of different devices: /device:TPU:39 before, /device:TPU:1 now
where the time goes in v1:
time: 103 us
  Pallas kernels  98.1 us (95%)
  local copies, waits for them, and re-layouts  4.29 us (4%)
    pallas_call x1, Pallas kernels, per_device(): pl.pallas_call(kernel, out_shape=(jax.ShapeDtypeStruct((ROWS, WIDTH), jnp...  98.1 us
    unnamed x7, local copies, waits for them, and re-layouts  4.29 us

profile of v1, /device:TPU:1, one launch (start us, length us, event | category | flops | bytes accessed | tf_op | source)
XLA Modules:
  0.0 103.0 jit_solution(10893991395138506901)
XLA Ops:
  0.6 0.0 copy-start
  0.6 0.7 copy-done
  1.3 0.0 copy-start.1
  1.3 0.7 copy-done.1
  2.0 98.1 %shard_map.58 = (bf16[400,4096]{1,0:T(8,128)(2,1)S(1)}, f32[1,400]{1,0:T(1,128)S(1)}, bf16[16,4096]{1,0:T(8,128)(2,1)S(1)}) custom-call(f32[1,6400,256]{2,1,0:T(8,128)} %master_hbm.1, f32[1,256]{1,0:T(1,128)S(1)} %bitcast.6, f32[1,256]{1,0:T(1,128)S(1)} %bitcast.7), custom_call_target="tpu_custom_call" | custom-call | tf_op jit(solution)/shard_map/pallas_call | solution.py:170
  100.1 1.7 %copy.9 = bf16[1,400,4096]{2,1,0:T(8,128)(2,1)} copy(bf16[1,400,4096]{2,1,0:T(8,128)(2,1)S(1)} %bitcast.4) | data formatting | bytes 6553600
  101.8 0.6 copy.10
  102.3 0.7 copy.11
Async XLA Ops:
  0.6 0.7 copy-start
  1.3 0.7 copy-start.1

commit v2 on v1

v2 whole, which is shorter than its diff:
```python
import jax
import jax.numpy as jnp
from jax import lax
from jax.experimental import pallas as pl
from jax.experimental.pallas import tpu as pltpu
from jax.sharding import PartitionSpec as P

MESH = pl.DeviceIdType.MESH
N = 16
HALF = 8
ROWS = 400
COLS = 256
WIDTH = 4096
TILES = ROWS // 8
RAW = 0

FAR = [(1, dx, dc) for dx in (0, 2, 1, 3) for dc in (0, 1)]
NEAR = [(0, dx, dc) for dx in (2, 1, 3) for dc in (0, 1)] + [(0, 0, 1)]
PEERS = FAR + NEAR
BACK = [NEAR.index((h, (4 - dx) % 4, dc)) for h, dx, dc in NEAR]
OWNERS = [(dz, dy) for dz in range(4) for dy in range(4)][1:]


def peer_row(me, step):
    half, dx, dc = step
    x = lax.rem(lax.rem(me // 2, 4) + dx, 4)
    return lax.rem(me // 8 + half, 2) * 8 + x * 2 + lax.rem(lax.rem(me, 2) + dc, 2)


def peer_owner(me, step):
    return lax.rem(me // 4 + step[0], 4) * 4 + lax.rem(lax.rem(me, 4) + step[1], 4)


def sums_of(block, at):
    part = jnp.sum(jnp.abs(block), axis=1, keepdims=True).reshape(TILES, 8, 1)
    shape = (TILES, 8, 128)
    place = lax.broadcasted_iota(jnp.int32, shape, 0) + at == lax.broadcasted_iota(jnp.int32, shape, 2)
    return jnp.sum(jnp.where(place, part, 0.0), axis=0)


def scaled(block, inverse, k):
    by = jnp.concatenate(
        [jnp.broadcast_to(inverse[:, c : c + 1], (8, COLS)) for c in (2 * k, 2 * k + 1)], axis=0
    )
    return (block * by).astype(jnp.bfloat16)


def kernel(
    master_hbm, product, final, scale, router,
    master, narrow, sums, parts, totals, raw, row, column,
    in_sem, part_s, part_r, total_s, total_r, tile_s, tile_r, row_s, row_r, pair_s, pair_r, half_s, half_r, raw_s, raw_r,
):
    me, owner = lax.axis_index("rows"), lax.axis_index("owner")
    rows_of = [peer_row(me, step) for step in PEERS]
    owners_of = [peer_owner(owner, step) for step in OWNERS]
    across = rows_of[0]
    pair_of = lambda device: lax.rem(device, HALF)

    def send(src, dst, send_sem, recv_sem, to_owner, to_row):
        copy = pltpu.make_async_remote_copy(
            src_ref=src, dst_ref=dst, send_sem=send_sem, recv_sem=recv_sem,
            device_id=(to_owner, to_row), device_id_type=MESH,
        )
        copy.start()
        return copy

    def columns_at(device):
        return pl.ds(pl.multiple_of(device * COLS, COLS), COLS)

    loads = []
    for d in range(N):
        load = pltpu.make_async_copy(
            master_hbm.at[0, pl.ds(d * ROWS, ROWS), :], master.at[pl.ds(d * ROWS, ROWS), :], in_sem.at[d]
        )
        load.start()
        loads.append(load)

    barrier = pltpu.get_barrier_semaphore()
    for r in rows_of:
        pl.semaphore_signal(barrier, inc=1, device_id=(owner, r), device_id_type=MESH)
    for o in owners_of:
        pl.semaphore_signal(barrier, inc=1, device_id=(o, me), device_id_type=MESH)

    row[...] = product[...][None]
    held = {}
    for d in range(N):
        loads[d].wait()
        held[d] = sums_of(master[pl.ds(d * ROWS, ROWS), :], 0 if d < HALF else TILES)
        if d >= HALF:
            sums[d - HALF] = held[d - HALF] + held[d]
    pl.semaphore_wait(barrier, len(rows_of) + len(owners_of))

    part_copies = [
        send(sums.at[pair_of(r)], parts.at[me], part_s.at[i], part_r.at[i], owner, r) for i, r in enumerate(rows_of)
    ]
    row_copies = [
        send(row.at[0], column.at[owner], row_s.at[i], row_r.at[i], o, me) for i, o in enumerate(owners_of)
    ]
    raw_copies = []
    if RAW:
        raw_copies.append(
            send(
                master.at[pl.ds(pl.multiple_of(across * ROWS, ROWS), RAW), :], raw, raw_s.at[0], raw_r.at[0], owner, across
            )
        )
    parts[me] = sums[pair_of(me)]
    column[owner] = row[0]
    for copy in part_copies:
        copy.wait_recv()
    total = parts[0]
    for d in range(1, N):
        total = total + parts[d]
    totals[pair_of(me)] = total / WIDTH
    total_copies = [
        send(
            totals.at[pair_of(me)], totals.at[pair_of(me)], total_s.at[i], total_r.at[i], owner, rows_of[len(FAR) + i]
        )
        for i in range(len(NEAR))
    ]

    def mean_of(device):
        both = totals[pair_of(device)]
        return jnp.where(device // HALF == 1, pltpu.roll(both, 128 - TILES, 1), both)

    def inverse_of(device):
        return 1.0 / jnp.where(lax.broadcasted_iota(jnp.int32, (8, 128), 1) < TILES, mean_of(device), 1.0)

    tile_copies = []

    def send_tile(i):
        device, first = rows_of[i], RAW if i == 0 else 0
        inverse = inverse_of(device)
        for k in range(first // 16, ROWS // 16):
            at = pl.ds(pl.multiple_of(device * ROWS + 16 * k, 16), 16)
            narrow[at, :] = scaled(master[at, :], inverse, k)
        tile_copies.append(
            send(
                narrow.at[pl.ds(pl.multiple_of(device * ROWS + first, 16), ROWS - first), :],
                final.at[pl.ds(first, ROWS - first), columns_at(me)],
                tile_s.at[i], tile_r.at[i], owner, device,
            )
        )

    arrived = set()

    def have_total(i):
        near = NEAR.index((0,) + PEERS[i][1:]) if PEERS[i][1:] != (0, 0) else None
        if near is not None and near not in arrived:
            total_copies[BACK[near]].wait_recv()
            arrived.add(near)

    for i in range(len(PEERS)):
        have_total(i)
        send_tile(i)
        if i == 1:
            for copy in row_copies:
                copy.wait_recv()
            router[:, columns_at(me)] = jnp.concatenate([column[o] for o in range(N)], axis=0).astype(jnp.bfloat16)
        if i == 2:
            pair = send(
                router.at[:, columns_at(me)], router.at[:, columns_at(me)], pair_s.at[0], pair_r.at[0], owner, across
            )

    own = inverse_of(me)
    for k in range(ROWS // 16):
        block = master[pl.ds(pl.multiple_of(me * ROWS + 16 * k, 16), 16), :]
        final[16 * k : 16 * k + 16, columns_at(me)] = scaled(block, own, k)

    shape = (128, 512)
    spread = (lax.broadcasted_iota(jnp.int32, shape, 1) // 8 == lax.broadcasted_iota(jnp.int32, shape, 0)).astype(jnp.float32)
    wide = jnp.dot(mean_of(me), spread, precision=lax.Precision.HIGHEST, preferred_element_type=jnp.float32)
    shape = (8, 512)
    keep = lax.rem(lax.broadcasted_iota(jnp.int32, shape, 1), 8) == lax.broadcasted_iota(jnp.int32, shape, 0)
    scale[...] = jnp.sum(jnp.where(keep, wide, 0.0), axis=0, keepdims=True)[:, :ROWS]

    for copy in raw_copies:
        copy.wait_recv()
        for k in range(RAW // 16):
            final[16 * k : 16 * k + 16, columns_at(across)] = scaled(raw[16 * k : 16 * k + 16, :], own, k)

    pair.wait_recv()
    half_copies = []
    for j in range(len(NEAR)):
        for k, block in enumerate((me, across)):
            half_copies.append(
                send(
                    router.at[:, columns_at(block)], router.at[:, columns_at(block)],
                    half_s.at[j, k], half_r.at[j, k], owner, rows_of[len(FAR) + j],
                )
            )
    for copy in part_copies + row_copies + total_copies + raw_copies + [pair]:
        copy.wait_send()
    for copy in half_copies + tile_copies:
        copy.wait()


def put(a, b, c, out_a, out_b, out_c, sem):
    copies = [pltpu.make_async_copy(src, dst, sem.at[i]) for i, (src, dst) in enumerate(((a, out_a), (b, out_b), (c, out_c)))]
    for copy in copies:
        copy.start()
    for copy in copies:
        copy.wait()


def per_device(master_down, router_weight, router_gain):
    vmem, hbm = pl.BlockSpec(memory_space=pltpu.VMEM), pl.BlockSpec(memory_space=pl.ANY)
    dma = pltpu.SemaphoreType.DMA
    peers, near, owners = len(PEERS), len(NEAR), len(OWNERS)
    outs = (
        jax.ShapeDtypeStruct((ROWS, WIDTH), jnp.bfloat16),
        jax.ShapeDtypeStruct((1, ROWS), jnp.float32),
        jax.ShapeDtypeStruct((N, WIDTH), jnp.bfloat16),
    )
    product = (router_weight * router_gain[:, None]).reshape(1, COLS)
    found = pl.pallas_call(
        kernel,
        out_shape=outs,
        in_specs=[hbm, vmem],
        out_specs=(vmem, vmem, vmem),
        scratch_shapes=[
            pltpu.VMEM((N * ROWS, COLS), jnp.float32),
            pltpu.VMEM((N * ROWS, COLS), jnp.bfloat16),
            pltpu.VMEM((HALF, 8, 128), jnp.float32),
            pltpu.VMEM((N, 8, 128), jnp.float32),
            pltpu.VMEM((HALF, 8, 128), jnp.float32),
            pltpu.VMEM((max(RAW, 16), COLS), jnp.float32),
            pltpu.VMEM((1, 1, COLS), jnp.float32),
            pltpu.VMEM((N, 1, COLS), jnp.float32),
            dma((N,)),
            dma((peers,)), dma((peers,)),
            dma((near,)), dma((near,)),
            dma((peers,)), dma((peers,)),
            dma((owners,)), dma((owners,)),
            dma((1,)), dma((1,)),
            dma((near, 2)), dma((near, 2)),
            dma((1,)), dma((1,)),
        ],
        compiler_params=pltpu.CompilerParams(
            collective_id=0, has_side_effects=True, vmem_limit_bytes=48 << 20
        ),
    )(master_down, product)
    final, scale, router = pl.pallas_call(
        put,
        out_shape=outs,
        in_specs=[vmem, vmem, vmem],
        out_specs=(hbm, hbm, hbm),
        scratch_shapes=[dma((3,))],
        compiler_params=pltpu.CompilerParams(vmem_limit_bytes=4 << 20),
    )(*found)
    return final[None], scale, router.T


def solution(mesh):
    return jax.shard_map(
        per_device,
        mesh=mesh,
        in_specs=(P("owner", None, "rows"), P("rows", "owner"), P("rows")),
        out_specs=(P("owner", "rows", None), P("owner", "rows"), P()),
        check_vma=False,
    )
```

time: 103 us -> 95.8 us (0.930)
  the two profiles are of different devices: /device:TPU:1 before, /device:TPU:13 now
where the time goes in v2:
time: 95.8 us; the launch traced here: 95.7 us
  Pallas kernels  94.4 us (99%)
    pallas_call x1, Pallas kernels, per_device(): pl.pallas_call(kernel, out_shape=outs, in_specs=[hbm, vmem], out_specs=(v...  92.6 us

profile of v2, /device:TPU:13, one launch (start us, length us, event | category | flops | bytes accessed | tf_op | source)
XLA Modules:
  0.0 95.7 jit_solution(231755944636454923)
XLA Ops:
  0.6 0.7 multiply_bitcast_fusion.product
  1.3 92.6 %shard_map.58 = (bf16[400,4096]{1,0:T(8,128)(2,1)S(1)}, f32[1,400]{1,0:T(1,128)S(1)}, bf16[16,4096]{1,0:T(8,128)(2,1)S(1)}) custom-call(f32[1,6400,256]{2,1,0:T(8,128)} %master_hbm.1, f32[1,256]{1,0:T(1,128)S(1)} %multiply_bitcast_fusion.product), custom_call_target="tpu_custom_call" | custom-call | tf_op jit(solution)/shard_map/pallas_call | solution.py:215
  94.0 1.8 %shard_map.59 = (bf16[400,4096]{1,0:T(8,128)(2,1)}, f32[1,400]{1,0:T(1,128)}, bf16[16,4096]{1,0:T(8,128)(2,1)}) custom-call(bf16[400,4096]{1,0:T(8,128)(2,1)S(1)} %get-tuple-element.9.a, f32[1,400]{1,0:T(1,128)S(1)} %get-tuple-element.10.b, bf16[16,4096]{1,0:T(8,128)(2,1)S(1)} %get-tuple-element.11.c), custom_call_target="tpu_custom_call" | custom-call | tf_op jit(solution)/shard_map/pallas_call | solution.py:242

commit v3 on v2

v3 whole, which is shorter than its diff:
```python
import jax
import jax.numpy as jnp
from jax import lax
from jax.experimental import pallas as pl
from jax.experimental.pallas import tpu as pltpu
from jax.sharding import PartitionSpec as P

MESH = pl.DeviceIdType.MESH
N = 16
HALF = 8
ROWS = 400
COLS = 256
WIDTH = 4096
TILES = ROWS // 8

FAR = [(1, dx, dc) for dx in (0, 2, 1, 3) for dc in (0, 1)]
NEAR = [(0, dx, dc) for dx in (2, 1, 3) for dc in (0, 1)] + [(0, 0, 1)]
PEERS = FAR + NEAR
BACK = [NEAR.index((h, (4 - dx) % 4, dc)) for h, dx, dc in NEAR]
PAIRS = [(dx, dc) for dx in (2, 1, 3, 0) for dc in (1, 0)]
QUAD = 4
FIRST = 208


def peer_row(me, step):
    half, dx, dc = step
    x = lax.rem(lax.rem(me // 2, 4) + dx, 4)
    return lax.rem(me // 8 + half, 2) * 8 + x * 2 + lax.rem(lax.rem(me, 2) + dc, 2)


def sums_of(block, at):
    part = jnp.sum(jnp.abs(block), axis=1, keepdims=True).reshape(TILES, 8, 1)
    shape = (TILES, 8, 128)
    place = lax.broadcasted_iota(jnp.int32, shape, 0) + at == lax.broadcasted_iota(jnp.int32, shape, 2)
    return jnp.sum(jnp.where(place, part, 0.0), axis=0)


def scaled(block, inverse, k):
    by = jnp.concatenate(
        [jnp.broadcast_to(inverse[:, c : c + 1], (8, COLS)) for c in (2 * k, 2 * k + 1)], axis=0
    )
    return (block * by).astype(jnp.bfloat16)


def kernel(
    master_hbm, weight_hbm, gain_hbm, final, scale, router,
    master, narrow, landed, sums, parts, totals, weight, gain, row, quad, column,
    in_sem, small_sem, part_s, part_r, total_s, total_r, tile_s, tile_r, land_s, land_r, on_s, on_r, across_s, across_r, quad_s, quad_r, column_s, column_r, pair_s, pair_r, half_s, half_r,
):
    me, owner = lax.axis_index("rows"), lax.axis_index("owner")
    rows_of = [peer_row(me, step) for step in PEERS]
    across = rows_of[0]
    deep, wide = owner // QUAD, lax.rem(owner, QUAD)
    along_wide = [deep * QUAD + lax.rem(wide + k, QUAD) for k in range(1, QUAD)]
    along_deep = [lax.rem(deep + k, QUAD) * QUAD + wide for k in range(1, QUAD)]
    pair_of = lambda device: lax.rem(device, HALF)

    def send(src, dst, send_sem, recv_sem, to_owner, to_row):
        copy = pltpu.make_async_remote_copy(
            src_ref=src, dst_ref=dst, send_sem=send_sem, recv_sem=recv_sem,
            device_id=(to_owner, to_row), device_id_type=MESH,
        )
        copy.start()
        return copy

    def columns_at(device):
        return pl.ds(pl.multiple_of(device * COLS, COLS), COLS)

    def tile_at(device):
        return pl.ds(pl.multiple_of(device * ROWS, 16), ROWS)

    smalls = [
        pltpu.make_async_copy(src, dst, small_sem.at[i])
        for i, (src, dst) in enumerate(((weight_hbm, weight), (gain_hbm, gain)))
    ]
    for small in smalls:
        small.start()
    loads = []
    for j, (dx, dc) in enumerate(PAIRS):
        q = pair_of(peer_row(me, (0, dx, dc)))
        for h in range(2):
            load = pltpu.make_async_copy(
                master_hbm.at[0, tile_at(q + HALF * h), :], master.at[tile_at(q + HALF * h), :], in_sem.at[j, h]
            )
            load.start()
            loads.append(load)

    barrier = pltpu.get_barrier_semaphore()
    for r in rows_of:
        pl.semaphore_signal(barrier, inc=1, device_id=(owner, r), device_id_type=MESH)
    for o in along_wide + along_deep:
        pl.semaphore_signal(barrier, inc=1, device_id=(o, me), device_id_type=MESH)
    for small in smalls:
        small.wait()
    row[...] = weight[...] * gain[...]
    quad[wide] = weight[...] * gain[...]
    pl.semaphore_wait(barrier, len(rows_of) + 2 * (QUAD - 1))

    quad_copies = [
        send(row, quad.at[wide], quad_s.at[i], quad_r.at[i], o, me) for i, o in enumerate(along_wide)
    ]
    part_copies = []
    for j, (dx, dc) in enumerate(PAIRS):
        q = pair_of(peer_row(me, (0, dx, dc)))
        for h in range(2):
            loads[2 * j + h].wait()
        sums[j] = sums_of(master[tile_at(q), :], 0) + sums_of(master[tile_at(q + HALF), :], TILES)
        if (dx, dc) == (0, 0):
            parts[me] = sums[j]
        for h in (1, 0):
            if (h, dx, dc) in PEERS:
                i = PEERS.index((h, dx, dc))
                part_copies.append(send(sums.at[j], parts.at[me], part_s.at[i], part_r.at[i], owner, rows_of[i]))
    for copy in quad_copies:
        copy.wait_recv()
    column[deep] = quad[...]
    column_copies = [
        send(quad, column.at[deep], column_s.at[i], column_r.at[i], o, me) for i, o in enumerate(along_deep)
    ]
    for copy in part_copies:
        copy.wait_recv()
    total = parts[0]
    for d in range(1, N):
        total = total + parts[d]
    totals[pair_of(me)] = total / WIDTH
    total_copies = [
        send(
            totals.at[pair_of(me)], totals.at[pair_of(me)], total_s.at[i], total_r.at[i], owner, rows_of[len(FAR) + i]
        )
        for i in range(len(NEAR))
    ]

    def mean_of(device):
        both = totals[pair_of(device)]
        return jnp.where(device // HALF == 1, pltpu.roll(both, 128 - TILES, 1), both)

    def inverse_of(device):
        return 1.0 / jnp.where(lax.broadcasted_iota(jnp.int32, (8, 128), 1) < TILES, mean_of(device), 1.0)

    def scale_tile(device, first, last):
        inverse = inverse_of(device)
        for k in range(first // 16, last // 16):
            at = pl.ds(pl.multiple_of(device * ROWS + 16 * k, 16), 16)
            narrow[at, :] = scaled(master[at, :], inverse, k)

    def send_across(s, first, last):
        scale_tile(across, first, last)
        rows = pl.ds(pl.multiple_of(across * ROWS + first, 16), last - first)
        return send(
            narrow.at[rows, :], final.at[pl.ds(first, last - first), columns_at(me)], across_s.at[s], across_r.at[s], owner, across
        )

    across_copies = [send_across(0, 0, FIRST)]
    for copy in column_copies:
        copy.wait_recv()
    block = jnp.concatenate([column[o // QUAD, o % QUAD] for o in range(N)], axis=0)
    router[:, columns_at(me)] = block.astype(jnp.bfloat16)
    land_copies = []
    for j, (_, dx, dc) in enumerate(NEAR):
        total_copies[BACK[j]].wait_recv()
        device = peer_row(me, (1, dx, dc))
        scale_tile(device, 0, ROWS)
        land_copies.append(send(narrow.at[tile_at(device), :], landed.at[j], land_s.at[j], land_r.at[j], owner, across))
        if j == 1:
            pair = send(
                router.at[:, columns_at(me)], router.at[:, columns_at(me)], pair_s.at[0], pair_r.at[0], owner, across
            )
    across_copies.append(send_across(1, FIRST, ROWS))
    tile_copies = []
    for j, (_, dx, dc) in enumerate(NEAR):
        device = peer_row(me, (0, dx, dc))
        scale_tile(device, 0, ROWS)
        tile_copies.append(
            send(narrow.at[tile_at(device), :], final.at[:, columns_at(me)], tile_s.at[j], tile_r.at[j], owner, device)
        )

    own = inverse_of(me)
    for k in range(ROWS // 16):
        block = master[pl.ds(pl.multiple_of(me * ROWS + 16 * k, 16), 16), :]
        final[16 * k : 16 * k + 16, columns_at(me)] = scaled(block, own, k)

    shape = (128, 512)
    spread = (lax.broadcasted_iota(jnp.int32, shape, 1) // 8 == lax.broadcasted_iota(jnp.int32, shape, 0)).astype(jnp.float32)
    wide = jnp.dot(mean_of(me), spread, precision=lax.Precision.HIGHEST, preferred_element_type=jnp.float32)
    shape = (8, 512)
    keep = lax.rem(lax.broadcasted_iota(jnp.int32, shape, 1), 8) == lax.broadcasted_iota(jnp.int32, shape, 0)
    scale[...] = jnp.sum(jnp.where(keep, wide, 0.0), axis=0, keepdims=True)[:, :ROWS]

    half_copies, on_copies = [], []
    for j, (_, dx, dc) in enumerate(NEAR):
        if j == 3:
            pair.wait_recv()
            for n in range(len(NEAR)):
                for k, device in enumerate((me, across)):
                    half_copies.append(
                        send(
                            router.at[:, columns_at(device)], router.at[:, columns_at(device)],
                            half_s.at[n, k], half_r.at[n, k], owner, rows_of[len(FAR) + n],
                        )
                    )
        land_copies[j].wait_recv()
        on_copies.append(
            send(
                landed.at[j], final.at[:, columns_at(across)], on_s.at[j], on_r.at[j], owner, rows_of[len(FAR) + j]
            )
        )
    for copy in quad_copies + column_copies + part_copies + total_copies + land_copies + [pair]:
        copy.wait_send()
    for copy in half_copies + tile_copies + on_copies + across_copies:
        copy.wait()


def put(a, b, c, out_a, out_b, out_c, sem):
    copies = [pltpu.make_async_copy(src, dst, sem.at[i]) for i, (src, dst) in enumerate(((a, out_a), (b, out_b), (c, out_c)))]
    for copy in copies:
        copy.start()
    for copy in copies:
        copy.wait()


def per_device(master_down, router_weight, router_gain):
    vmem, hbm = pl.BlockSpec(memory_space=pltpu.VMEM), pl.BlockSpec(memory_space=pl.ANY)
    dma = pltpu.SemaphoreType.DMA
    peers, near = len(PEERS), len(NEAR)
    outs = (
        jax.ShapeDtypeStruct((ROWS, WIDTH), jnp.bfloat16),
        jax.ShapeDtypeStruct((1, ROWS), jnp.float32),
        jax.ShapeDtypeStruct((N, WIDTH), jnp.bfloat16),
    )
    small = [
        pltpu.with_memory_space_constraint(a.reshape(1, COLS), pltpu.HBM) for a in (router_weight, router_gain)
    ]
    found = pl.pallas_call(
        kernel,
        out_shape=outs,
        in_specs=[hbm, hbm, hbm],
        out_specs=(vmem, vmem, vmem),
        scratch_shapes=[
            pltpu.VMEM((N * ROWS, COLS), jnp.float32),
            pltpu.VMEM((N * ROWS, COLS), jnp.bfloat16),
            pltpu.VMEM((len(NEAR), ROWS, COLS), jnp.bfloat16),
            pltpu.VMEM((HALF, 8, 128), jnp.float32),
            pltpu.VMEM((N, 8, 128), jnp.float32),
            pltpu.VMEM((HALF, 8, 128), jnp.float32),
            pltpu.VMEM((1, COLS), jnp.float32),
            pltpu.VMEM((1, COLS), jnp.float32),
            pltpu.VMEM((1, COLS), jnp.float32),
            pltpu.VMEM((QUAD, 1, COLS), jnp.float32),
            pltpu.VMEM((QUAD, QUAD, 1, COLS), jnp.float32),
            dma((HALF, 2)),
            dma((2,)),
            dma((peers,)), dma((peers,)),
            dma((near,)), dma((near,)),
            dma((near,)), dma((near,)),
            dma((near,)), dma((near,)),
            dma((near,)), dma((near,)),
            dma((2,)), dma((2,)),
            dma((QUAD - 1,)), dma((QUAD - 1,)),
            dma((QUAD - 1,)), dma((QUAD - 1,)),
            dma((1,)), dma((1,)),
            dma((near, 2)), dma((near, 2)),
        ],
        compiler_params=pltpu.CompilerParams(
            collective_id=0, has_side_effects=True, vmem_limit_bytes=50331648
        ),
    )(master_down, *small)
    final, scale, router = pl.pallas_call(
        put,
        out_shape=outs,
        in_specs=[vmem, vmem, vmem],
        out_specs=(hbm, hbm, hbm),
        scratch_shapes=[dma((3,))],
        compiler_params=pltpu.CompilerParams(vmem_limit_bytes=4 << 20),
    )(*found)
    return final[None], scale, router.T


def solution(mesh):
    return jax.shard_map(
        per_device,
        mesh=mesh,
        in_specs=(P("owner", None, "rows"), P("rows", "owner"), P("rows")),
        out_specs=(P("owner", "rows", None), P("owner", "rows"), P()),
        check_vma=False,
    )
```

time: 95.8 us -> 93.8 us (0.979)
  the two profiles are of different devices: /device:TPU:13 before, /device:TPU:35 now
where the time goes in v3:
time: 93.8 us; the launch traced here: 92.6 us
  Pallas kernels  91.9 us (98%)
    pallas_call x1, Pallas kernels, per_device(): pl.pallas_call(kernel, out_shape=outs, in_specs=[hbm, hbm, hbm], out_spec...  90.1 us

profile of v3, /device:TPU:35, one launch (start us, length us, event | category | flops | bytes accessed | tf_op | source)
XLA Modules:
  0.0 92.6 jit_solution(6889623507636375392)
XLA Ops:
  0.6 90.1 %shard_map.58 = (bf16[400,4096]{1,0:T(8,128)(2,1)S(1)}, f32[1,400]{1,0:T(1,128)S(1)}, bf16[16,4096]{1,0:T(8,128)(2,1)S(1)}) custom-call(f32[1,6400,256]{2,1,0:T(8,128)} %master_hbm.1, f32[1,256]{1,0:T(1,128)} %bitcast.4, f32[1,256]{1,0:T(1,128)} %bitcast.5), custom_call_target="tpu_custom_call" | custom-call | tf_op jit(solution)/shard_map/pallas_call | solution.py:233
  90.8 1.8 %shard_map.59 = (bf16[400,4096]{1,0:T(8,128)(2,1)}, f32[1,400]{1,0:T(1,128)}, bf16[16,4096]{1,0:T(8,128)(2,1)}) custom-call(bf16[400,4096]{1,0:T(8,128)(2,1)S(1)} %get-tuple-element.9.a, f32[1,400]{1,0:T(1,128)S(1)} %get-tuple-element.10.b, bf16[16,4096]{1,0:T(8,128)(2,1)S(1)} %get-tuple-element.11.c), custom_call_target="tpu_custom_call" | custom-call | tf_op jit(solution)/shard_map/pallas_call | solution.py:267

commit v4 on v3

--- a/solution.py
+++ b/solution.py
@@ -19,6 +19,7 @@
 BACK = [NEAR.index((h, (4 - dx) % 4, dc)) for h, dx, dc in NEAR]
 PAIRS = [(dx, dc) for dx in (2, 1, 3, 0) for dc in (1, 0)]
 QUAD = 4
+RAW = 112
 FIRST = 208
 
 
@@ -44,12 +45,13 @@
 
 def kernel(
     master_hbm, weight_hbm, gain_hbm, final, scale, router,
-    master, narrow, landed, sums, parts, totals, weight, gain, row, quad, column,
-    in_sem, small_sem, part_s, part_r, total_s, total_r, tile_s, tile_r, land_s, land_r, on_s, on_r, across_s, across_r, quad_s, quad_r, column_s, column_r, pair_s, pair_r, half_s, half_r,
+    master, narrow, landed, raw, sums, parts, totals, weight, gain, row, column, blocks,
+    in_sem, small_sem, part_s, part_r, total_s, total_r, tile_s, tile_r, land_s, land_r, on_s, on_r, across_s, across_r, raw_s, raw_r, column_s, column_r, block_s, block_r, pair_s, pair_r, half_s, half_r,
 ):
     me, owner = lax.axis_index("rows"), lax.axis_index("owner")
     rows_of = [peer_row(me, step) for step in PEERS]
     across = rows_of[0]
+    upper = me // HALF
     deep, wide = owner // QUAD, lax.rem(owner, QUAD)
     along_wide = [deep * QUAD + lax.rem(wide + k, QUAD) for k in range(1, QUAD)]
     along_deep = [lax.rem(deep + k, QUAD) * QUAD + wide for k in range(1, QUAD)]
@@ -93,11 +95,11 @@
     for small in smalls:
         small.wait()
     row[...] = weight[...] * gain[...]
-    quad[wide] = weight[...] * gain[...]
+    column[upper, deep] = weight[...] * gain[...]
     pl.semaphore_wait(barrier, len(rows_of) + 2 * (QUAD - 1))
 
-    quad_copies = [
-        send(row, quad.at[wide], quad_s.at[i], quad_r.at[i], o, me) for i, o in enumerate(along_wide)
+    column_copies = [
+        send(row, column.at[upper, deep], column_s.at[i], column_r.at[i], o, me) for i, o in enumerate(along_deep)
     ]
     part_copies = []
     for j, (dx, dc) in enumerate(PAIRS):
@@ -111,12 +113,12 @@
             if (h, dx, dc) in PEERS:
                 i = PEERS.index((h, dx, dc))
                 part_copies.append(send(sums.at[j], parts.at[me], part_s.at[i], part_r.at[i], owner, rows_of[i]))
-    for copy in quad_copies:
+    for copy in column_copies:
         copy.wait_recv()
-    column[deep] = quad[...]
-    column_copies = [
-        send(quad, column.at[deep], column_s.at[i], column_r.at[i], o, me) for i, o in enumerate(along_deep)
-    ]
+    pair = send(column.at[upper], column.at[upper], pair_s.at[0], pair_r.at[0], owner, across)
+    raw_copy = send(
+        master.at[pl.ds(pl.multiple_of(across * ROWS, 16), RAW), :], raw, raw_s.at[0], raw_r.at[0], owner, across
+    )
     for copy in part_copies:
         copy.wait_recv()
     total = parts[0]
@@ -150,21 +152,13 @@
             narrow.at[rows, :], final.at[pl.ds(first, last - first), columns_at(me)], across_s.at[s], across_r.at[s], owner, across
         )
 
-    across_copies = [send_across(0, 0, FIRST)]
-    for copy in column_copies:
-        copy.wait_recv()
-    block = jnp.concatenate([column[o // QUAD, o % QUAD] for o in range(N)], axis=0)
-    router[:, columns_at(me)] = block.astype(jnp.bfloat16)
+    across_copies = [send_across(0, RAW, FIRST)]
     land_copies = []
     for j, (_, dx, dc) in enumerate(NEAR):
         total_copies[BACK[j]].wait_recv()
         device = peer_row(me, (1, dx, dc))
         scale_tile(device, 0, ROWS)
         land_copies.append(send(narrow.at[tile_at(device), :], landed.at[j], land_s.at[j], land_r.at[j], owner, across))
-        if j == 1:
-            pair = send(
-                router.at[:, columns_at(me)], router.at[:, columns_at(me)], pair_s.at[0], pair_r.at[0], owner, across
-            )
     across_copies.append(send_across(1, FIRST, ROWS))
     tile_copies = []
     for j, (_, dx, dc) in enumerate(NEAR):
@@ -179,6 +173,16 @@
         block = master[pl.ds(pl.multiple_of(me * ROWS + 16 * k, 16), 16), :]
         final[16 * k : 16 * k + 16, columns_at(me)] = scaled(block, own, k)
 
+    raw_copy.wait_recv()
+    for k in range(RAW // 16):
+        final[16 * k : 16 * k + 16, columns_at(across)] = scaled(raw[16 * k : 16 * k + 16, :], own, k)
+
+    pair.wait_recv()
+    blocks[wide] = column[...]
+    block_copies = [
+        send(column, blocks.at[wide], block_s.at[i], block_r.at[i], o, me) for i, o in enumerate(along_wide)
+    ]
+
     shape = (128, 512)
     spread = (lax.broadcasted_iota(jnp.int32, shape, 1) // 8 == lax.broadcasted_iota(jnp.int32, shape, 0)).astype(jnp.float32)
     wide = jnp.dot(mean_of(me), spread, precision=lax.Precision.HIGHEST, preferred_element_type=jnp.float32)
@@ -186,25 +190,27 @@
     keep = lax.rem(lax.broadcasted_iota(jnp.int32, shape, 1), 8) == lax.broadcasted_iota(jnp.int32, shape, 0)
     scale[...] = jnp.sum(jnp.where(keep, wide, 0.0), axis=0, keepdims=True)[:, :ROWS]
 
-    half_copies, on_copies = [], []
-    for j, (_, dx, dc) in enumerate(NEAR):
-        if j == 3:
-            pair.wait_recv()
-            for n in range(len(NEAR)):
-                for k, device in enumerate((me, across)):
-                    half_copies.append(
-                        send(
-                            router.at[:, columns_at(device)], router.at[:, columns_at(device)],
-                            half_s.at[n, k], half_r.at[n, k], owner, rows_of[len(FAR) + n],
-                        )
-                    )
+    for copy in block_copies:
+        copy.wait_recv()
+    half_copies = []
+    for h in range(2):
+        lines = [blocks[o % QUAD, h, o // QUAD] for o in range(N)]
+        at = columns_at(h * HALF + pair_of(me))
+        router[:, at] = jnp.concatenate(lines, axis=0).astype(jnp.bfloat16)
+        for n in range(len(NEAR)):
+            half_copies.append(
+                send(router.at[:, at], router.at[:, at], half_s.at[n, h], half_r.at[n, h], owner, rows_of[len(FAR) + n])
+            )
+
+    on_copies = []
+    for j in range(len(NEAR)):
         land_copies[j].wait_recv()
         on_copies.append(
             send(
                 landed.at[j], final.at[:, columns_at(across)], on_s.at[j], on_r.at[j], owner, rows_of[len(FAR) + j]
             )
         )
-    for copy in quad_copies + column_copies + part_copies + total_copies + land_copies + [pair]:
+    for copy in block_copies + column_copies + part_copies + total_copies + land_copies + [pair, raw_copy]:
         copy.wait_send()
     for copy in half_copies + tile_copies + on_copies + across_copies:
         copy.wait()
@@ -239,14 +245,15 @@
             pltpu.VMEM((N * ROWS, COLS), jnp.float32),
             pltpu.VMEM((N * ROWS, COLS), jnp.bfloat16),
             pltpu.VMEM((len(NEAR), ROWS, COLS), jnp.bfloat16),
+            pltpu.VMEM((RAW, COLS), jnp.float32),
             pltpu.VMEM((HALF, 8, 128), jnp.float32),
             pltpu.VMEM((N, 8, 128), jnp.float32),
             pltpu.VMEM((HALF, 8, 128), jnp.float32),
             pltpu.VMEM((1, COLS), jnp.float32),
             pltpu.VMEM((1, COLS), jnp.float32),
             pltpu.VMEM((1, COLS), jnp.float32),
-            pltpu.VMEM((QUAD, 1, COLS), jnp.float32),
-            pltpu.VMEM((QUAD, QUAD, 1, COLS), jnp.float32),
+            pltpu.VMEM((2, QUAD, 1, COLS), jnp.float32),
+            pltpu.VMEM((QUAD, 2, QUAD, 1, COLS), jnp.float32),
             dma((HALF, 2)),
             dma((2,)),
             dma((peers,)), dma((peers,)),
@@ -255,6 +262,7 @@
             dma((near,)), dma((near,)),
             dma((near,)), dma((near,)),
             dma((2,)), dma((2,)),
+            dma((1,)), dma((1,)),
             dma((QUAD - 1,)), dma((QUAD - 1,)),
             dma((QUAD - 1,)), dma((QUAD - 1,)),
             dma((1,)), dma((1,)),

time: 93.8 us -> 91.9 us (0.980)
  Pallas kernels: 91.9 us -> 90.3 us
    pallas_call x1, Pallas kernels: 90.1 us -> 88.5 us  [per_device(): pl.pallas_call(kernel, out_shape=outs, in_specs=[hbm, hbm, hbm], out_spec...]
where the time goes in v4:
time: 91.9 us; the launch traced here: 90.9 us
  Pallas kernels  90.3 us (98%)
    pallas_call x1, Pallas kernels, per_device(): pl.pallas_call(kernel, out_shape=outs, in_specs=[hbm, hbm, hbm], out_spec...  88.5 us

profile of v4, /device:TPU:35, one launch (start us, length us, event | category | flops | bytes accessed | tf_op | source)
XLA Modules:
  0.0 90.9 jit_solution(11295364478612832074)
XLA Ops:
  0.6 88.5 %shard_map.58 = (bf16[400,4096]{1,0:T(8,128)(2,1)S(1)}, f32[1,400]{1,0:T(1,128)S(1)}, bf16[16,4096]{1,0:T(8,128)(2,1)S(1)}) custom-call(f32[1,6400,256]{2,1,0:T(8,128)} %master_hbm.1, f32[1,256]{1,0:T(1,128)} %bitcast.4, f32[1,256]{1,0:T(1,128)} %bitcast.5), custom_call_target="tpu_custom_call" | custom-call | tf_op jit(solution)/shard_map/pallas_call | solution.py:239
  89.1 1.8 %shard_map.59 = (bf16[400,4096]{1,0:T(8,128)(2,1)}, f32[1,400]{1,0:T(1,128)}, bf16[16,4096]{1,0:T(8,128)(2,1)}) custom-call(bf16[400,4096]{1,0:T(8,128)(2,1)S(1)} %get-tuple-element.9.a, f32[1,400]{1,0:T(1,128)S(1)} %get-tuple-element.10.b, bf16[16,4096]{1,0:T(8,128)(2,1)S(1)} %get-tuple-element.11.c), custom_call_target="tpu_custom_call" | custom-call | tf_op jit(solution)/shard_map/pallas_call | solution.py:275

commit v5 on v4

--- a/solution.py
+++ b/solution.py
@@ -20,6 +20,7 @@
 PAIRS = [(dx, dc) for dx in (2, 1, 3, 0) for dc in (1, 0)]
 QUAD = 4
 RAW = 112
+EARLY = 6
 FIRST = 208
 
 
@@ -96,17 +97,23 @@
         small.wait()
     row[...] = weight[...] * gain[...]
     column[upper, deep] = weight[...] * gain[...]
-    pl.semaphore_wait(barrier, len(rows_of) + 2 * (QUAD - 1))
-
-    column_copies = [
-        send(row, column.at[upper, deep], column_s.at[i], column_r.at[i], o, me) for i, o in enumerate(along_deep)
-    ]
-    part_copies = []
-    for j, (dx, dc) in enumerate(PAIRS):
+    def add_up(j, dx, dc):
         q = pair_of(peer_row(me, (0, dx, dc)))
         for h in range(2):
             loads[2 * j + h].wait()
         sums[j] = sums_of(master[tile_at(q), :], 0) + sums_of(master[tile_at(q + HALF), :], TILES)
+
+    for j in range(EARLY):
+        add_up(j, *PAIRS[j])
+    pl.semaphore_wait(barrier, len(rows_of) + 2 * (QUAD - 1))
+
+    column_copies = [
+        send(row, column.at[upper, deep], column_s.at[i], column_r.at[i], o, me) for i, o in enumerate(along_deep)
+    ]
+    part_copies = []
+    for j, (dx, dc) in enumerate(PAIRS):
+        if j >= EARLY:
+            add_up(j, dx, dc)
         if (dx, dc) == (0, 0):
             parts[me] = sums[j]
         for h in (1, 0):

time: 91.9 us -> 91.2 us (level); the launches traced: 90.9 us -> 91.1 us
  no operation moved by 1% of the time
where the time goes in v5:
time: 91.2 us; the launch traced here: 91.1 us
  Pallas kernels  90.5 us (99%)
    pallas_call x1, Pallas kernels, per_device(): pl.pallas_call(kernel, out_shape=outs, in_specs=[hbm, hbm, hbm], out_spec...  88.7 us

profile of v5, /device:TPU:35, one launch (start us, length us, event | category | flops | bytes accessed | tf_op | source)
XLA Modules:
  0.0 91.1 jit_solution(8813657523997913062)
XLA Ops:
  0.6 88.7 %shard_map.58 = (bf16[400,4096]{1,0:T(8,128)(2,1)S(1)}, f32[1,400]{1,0:T(1,128)S(1)}, bf16[16,4096]{1,0:T(8,128)(2,1)S(1)}) custom-call(f32[1,6400,256]{2,1,0:T(8,128)} %master_hbm.1, f32[1,256]{1,0:T(1,128)} %bitcast.4, f32[1,256]{1,0:T(1,128)} %bitcast.5), custom_call_target="tpu_custom_call" | custom-call | tf_op jit(solution)/shard_map/pallas_call | solution.py:246
  89.4 1.8 %shard_map.59 = (bf16[400,4096]{1,0:T(8,128)(2,1)}, f32[1,400]{1,0:T(1,128)}, bf16[16,4096]{1,0:T(8,128)(2,1)}) custom-call(bf16[400,4096]{1,0:T(8,128)(2,1)S(1)} %get-tuple-element.9.a, f32[1,400]{1,0:T(1,128)S(1)} %get-tuple-element.10.b, bf16[16,4096]{1,0:T(8,128)(2,1)S(1)} %get-tuple-element.11.c), custom_call_target="tpu_custom_call" | custom-call | tf_op jit(solution)/shard_map/pallas_call | solution.py:282

commit v6 on v5

--- a/solution.py
+++ b/solution.py
@@ -66,6 +66,9 @@
         copy.start()
         return copy
 
+    def settle(ref, sem):
+        pltpu.make_async_copy(ref, ref, sem).wait()
+
     def columns_at(device):
         return pl.ds(pl.multiple_of(device * COLS, COLS), COLS)
 
@@ -78,15 +81,13 @@
     ]
     for small in smalls:
         small.start()
-    loads = []
     for j, (dx, dc) in enumerate(PAIRS):
         q = pair_of(peer_row(me, (0, dx, dc)))
         for h in range(2):
             load = pltpu.make_async_copy(
-                master_hbm.at[0, tile_at(q + HALF * h), :], master.at[tile_at(q + HALF * h), :], in_sem.at[j, h]
+                master_hbm.at[0, tile_at(q + HALF * h), :], master.at[tile_at(q + HALF * h), :], in_sem.at[j]
             )
             load.start()
-            loads.append(load)
 
     barrier = pltpu.get_barrier_semaphore()
     for r in rows_of:
@@ -99,8 +100,7 @@
     column[upper, deep] = weight[...] * gain[...]
     def add_up(j, dx, dc):
         q = pair_of(peer_row(me, (0, dx, dc)))
-        for h in range(2):
-            loads[2 * j + h].wait()
+        settle(master.at[pl.ds(0, 2 * ROWS), :], in_sem.at[j])
         sums[j] = sums_of(master[tile_at(q), :], 0) + sums_of(master[tile_at(q + HALF), :], TILES)
 
     for j in range(EARLY):
@@ -108,7 +108,7 @@
     pl.semaphore_wait(barrier, len(rows_of) + 2 * (QUAD - 1))
 
     column_copies = [
-        send(row, column.at[upper, deep], column_s.at[i], column_r.at[i], o, me) for i, o in enumerate(along_deep)
+        send(row, column.at[upper, deep], column_s.at[0], column_r.at[0], o, me) for i, o in enumerate(along_deep)
     ]
     part_copies = []
     for j, (dx, dc) in enumerate(PAIRS):
@@ -119,22 +119,22 @@
         for h in (1, 0):
             if (h, dx, dc) in PEERS:
                 i = PEERS.index((h, dx, dc))
-                part_copies.append(send(sums.at[j], parts.at[me], part_s.at[i], part_r.at[i], owner, rows_of[i]))
-    for copy in column_copies:
-        copy.wait_recv()
+                part_copies.append(send(sums.at[j], parts.at[me], part_s.at[0], part_r.at[0], owner, rows_of[i]))
+    three = column.at[0, pl.ds(0, QUAD - 1)]
+    settle(three, column_r.at[0])
     pair = send(column.at[upper], column.at[upper], pair_s.at[0], pair_r.at[0], owner, across)
     raw_copy = send(
         master.at[pl.ds(pl.multiple_of(across * ROWS, 16), RAW), :], raw, raw_s.at[0], raw_r.at[0], owner, across
     )
-    for copy in part_copies:
-        copy.wait_recv()
+    fifteen = parts.at[pl.ds(0, N - 1)]
+    settle(fifteen, part_r.at[0])
     total = parts[0]
     for d in range(1, N):
         total = total + parts[d]
     totals[pair_of(me)] = total / WIDTH
     total_copies = [
         send(
-            totals.at[pair_of(me)], totals.at[pair_of(me)], total_s.at[i], total_r.at[i], owner, rows_of[len(FAR) + i]
+            totals.at[pair_of(me)], totals.at[pair_of(me)], total_s.at[0], total_r.at[i], owner, rows_of[len(FAR) + i]
         )
         for i in range(len(NEAR))
     ]
@@ -156,7 +156,7 @@
         scale_tile(across, first, last)
         rows = pl.ds(pl.multiple_of(across * ROWS + first, 16), last - first)
         return send(
-            narrow.at[rows, :], final.at[pl.ds(first, last - first), columns_at(me)], across_s.at[s], across_r.at[s], owner, across
+            narrow.at[rows, :], final.at[pl.ds(first, last - first), columns_at(me)], across_s.at[0], across_r.at[0], owner, across
         )
 
     across_copies = [send_across(0, RAW, FIRST)]
@@ -165,14 +165,14 @@
         total_copies[BACK[j]].wait_recv()
         device = peer_row(me, (1, dx, dc))
         scale_tile(device, 0, ROWS)
-        land_copies.append(send(narrow.at[tile_at(device), :], landed.at[j], land_s.at[j], land_r.at[j], owner, across))
+        land_copies.append(send(narrow.at[tile_at(device), :], landed.at[j], land_s.at[0], land_r.at[j], owner, across))
     across_copies.append(send_across(1, FIRST, ROWS))
     tile_copies = []
     for j, (_, dx, dc) in enumerate(NEAR):
         device = peer_row(me, (0, dx, dc))
         scale_tile(device, 0, ROWS)
         tile_copies.append(
-            send(narrow.at[tile_at(device), :], final.at[:, columns_at(me)], tile_s.at[j], tile_r.at[j], owner, device)
+            send(narrow.at[tile_at(device), :], final.at[:, columns_at(me)], tile_s.at[0], tile_r.at[0], owner, device)
         )
 
     own = inverse_of(me)
@@ -187,7 +187,7 @@
     pair.wait_recv()
     blocks[wide] = column[...]
     block_copies = [
-        send(column, blocks.at[wide], block_s.at[i], block_r.at[i], o, me) for i, o in enumerate(along_wide)
+        send(column, blocks.at[wide], block_s.at[0], block_r.at[0], o, me) for i, o in enumerate(along_wide)
     ]
 
     shape = (128, 512)
@@ -197,8 +197,8 @@
     keep = lax.rem(lax.broadcasted_iota(jnp.int32, shape, 1), 8) == lax.broadcasted_iota(jnp.int32, shape, 0)
     scale[...] = jnp.sum(jnp.where(keep, wide, 0.0), axis=0, keepdims=True)[:, :ROWS]
 
-    for copy in block_copies:
-        copy.wait_recv()
+    others = blocks.at[pl.ds(0, QUAD - 1)]
+    settle(others, block_r.at[0])
     half_copies = []
     for h in range(2):
         lines = [blocks[o % QUAD, h, o // QUAD] for o in range(N)]
@@ -206,7 +206,7 @@
         router[:, at] = jnp.concatenate(lines, axis=0).astype(jnp.bfloat16)
         for n in range(len(NEAR)):
             half_copies.append(
-                send(router.at[:, at], router.at[:, at], half_s.at[n, h], half_r.at[n, h], owner, rows_of[len(FAR) + n])
+                send(router.at[:, at], router.at[:, at], half_s.at[0], half_r.at[0], owner, rows_of[len(FAR) + n])
             )
 
     on_copies = []
@@ -214,13 +214,24 @@
         land_copies[j].wait_recv()
         on_copies.append(
             send(
-                landed.at[j], final.at[:, columns_at(across)], on_s.at[j], on_r.at[j], owner, rows_of[len(FAR) + j]
+                landed.at[j], final.at[:, columns_at(across)], on_s.at[0], on_r.at[0], owner, rows_of[len(FAR) + j]
             )
         )
-    for copy in block_copies + column_copies + part_copies + total_copies + land_copies + [pair, raw_copy]:
+    for copy in (pair, raw_copy):
         copy.wait_send()
-    for copy in half_copies + tile_copies + on_copies + across_copies:
-        copy.wait()
+    settle(three, column_s.at[0])
+    settle(fifteen, part_s.at[0])
+    settle(others, block_s.at[0])
+    settle(totals.at[pl.ds(0, len(NEAR))], total_s.at[0])
+    settle(landed, land_s.at[0])
+    across_part = narrow.at[pl.ds(0, ROWS - RAW), :]
+    settle(across_part, across_s.at[0])
+    router_part = router.at[:, pl.ds(0, 2 * len(NEAR) * COLS)]
+    settle(router_part, half_s.at[0])
+    settle(router_part, half_r.at[0])
+    for sem in (tile_s, tile_r, on_s, on_r):
+        settle(landed, sem.at[0])
+    settle(across_part, across_r.at[0])
 
 
 def put(a, b, c, out_a, out_b, out_c, sem):
@@ -234,7 +245,7 @@
 def per_device(master_down, router_weight, router_gain):
     vmem, hbm = pl.BlockSpec(memory_space=pltpu.VMEM), pl.BlockSpec(memory_space=pl.ANY)
     dma = pltpu.SemaphoreType.DMA
-    peers, near = len(PEERS), len(NEAR)
+    near = len(NEAR)
     outs = (
         jax.ShapeDtypeStruct((ROWS, WIDTH), jnp.bfloat16),
         jax.ShapeDtypeStruct((1, ROWS), jnp.float32),
@@ -261,19 +272,19 @@
             pltpu.VMEM((1, COLS), jnp.float32),
             pltpu.VMEM((2, QUAD, 1, COLS), jnp.float32),
             pltpu.VMEM((QUAD, 2, QUAD, 1, COLS), jnp.float32),
-            dma((HALF, 2)),
+            dma((HALF,)),
             dma((2,)),
-            dma((peers,)), dma((peers,)),
-            dma((near,)), dma((near,)),
-            dma((near,)), dma((near,)),
-            dma((near,)), dma((near,)),
-            dma((near,)), dma((near,)),
-            dma((2,)), dma((2,)),
-            dma((1,)), dma((1,)),
-            dma((QUAD - 1,)), dma((QUAD - 1,)),
-            dma((QUAD - 1,)), dma((QUAD - 1,)),
-            dma((1,)), dma((1,)),
-            dma((near, 2)), dma((near, 2)),
+            dma((1,)), dma((1,)),
+            dma((1,)), dma((near,)),
+            dma((1,)), dma((1,)),
+            dma((1,)), dma((near,)),
+            dma((1,)), dma((1,)),
+            dma((1,)), dma((1,)),
+            dma((1,)), dma((1,)),
+            dma((1,)), dma((1,)),
+            dma((1,)), dma((1,)),
+            dma((1,)), dma((1,)),
+            dma((1,)), dma((1,)),
         ],
         compiler_params=pltpu.CompilerParams(
             collective_id=0, has_side_effects=True, vmem_limit_bytes=50331648

time: 91.2 us -> 90.2 us (0.989)
  Pallas kernels: 90.5 us -> 89.5 us
    pallas_call x1, Pallas kernels: 88.7 us -> 87.7 us  [per_device(): pl.pallas_call(kernel, out_shape=outs, in_specs=[hbm, hbm, hbm], out_spec...]
where the time goes in v6:
time: 90.2 us; the launch traced here: 90.1 us
  Pallas kernels  89.5 us (99%)
    pallas_call x1, Pallas kernels, per_device(): pl.pallas_call(kernel, out_shape=outs, in_specs=[hbm, hbm, hbm], out_spec...  87.7 us

profile of v6, /device:TPU:35, one launch (start us, length us, event | category | flops | bytes accessed | tf_op | source)
XLA Modules:
  0.0 90.1 jit_solution(17007492356825766386)
XLA Ops:
  0.6 87.7 %shard_map.58 = (bf16[400,4096]{1,0:T(8,128)(2,1)S(1)}, f32[1,400]{1,0:T(1,128)S(1)}, bf16[16,4096]{1,0:T(8,128)(2,1)S(1)}) custom-call(f32[1,6400,256]{2,1,0:T(8,128)} %master_hbm.1, f32[1,256]{1,0:T(1,128)} %bitcast.4, f32[1,256]{1,0:T(1,128)} %bitcast.5), custom_call_target="tpu_custom_call" | custom-call | tf_op jit(solution)/shard_map/pallas_call | solution.py:257
  88.4 1.8 %shard_map.59 = (bf16[400,4096]{1,0:T(8,128)(2,1)}, f32[1,400]{1,0:T(1,128)}, bf16[16,4096]{1,0:T(8,128)(2,1)}) custom-call(bf16[400,4096]{1,0:T(8,128)(2,1)S(1)} %get-tuple-element.9.a, f32[1,400]{1,0:T(1,128)S(1)} %get-tuple-element.10.b, bf16[16,4096]{1,0:T(8,128)(2,1)S(1)} %get-tuple-element.11.c), custom_call_target="tpu_custom_call" | custom-call | tf_op jit(solution)/shard_map/pallas_call | solution.py:293

commit v7 on v6

--- a/solution.py
+++ b/solution.py
@@ -167,6 +167,15 @@
         scale_tile(device, 0, ROWS)
         land_copies.append(send(narrow.at[tile_at(device), :], landed.at[j], land_s.at[0], land_r.at[j], owner, across))
     across_copies.append(send_across(1, FIRST, ROWS))
+    own = inverse_of(me)
+    for k in range(ROWS // 16):
+        block = master[pl.ds(pl.multiple_of(me * ROWS + 16 * k, 16), 16), :]
+        final[16 * k : 16 * k + 16, columns_at(me)] = scaled(block, own, k)
+
+    raw_copy.wait_recv()
+    for k in range(RAW // 16):
+        final[16 * k : 16 * k + 16, columns_at(across)] = scaled(raw[16 * k : 16 * k + 16, :], own, k)
+
     tile_copies = []
     for j, (_, dx, dc) in enumerate(NEAR):
         device = peer_row(me, (0, dx, dc))
@@ -174,15 +183,6 @@
         tile_copies.append(
             send(narrow.at[tile_at(device), :], final.at[:, columns_at(me)], tile_s.at[0], tile_r.at[0], owner, device)
         )
-
-    own = inverse_of(me)
-    for k in range(ROWS // 16):
-        block = master[pl.ds(pl.multiple_of(me * ROWS + 16 * k, 16), 16), :]
-        final[16 * k : 16 * k + 16, columns_at(me)] = scaled(block, own, k)
-
-    raw_copy.wait_recv()
-    for k in range(RAW // 16):
-        final[16 * k : 16 * k + 16, columns_at(across)] = scaled(raw[16 * k : 16 * k + 16, :], own, k)
 
     pair.wait_recv()
     blocks[wide] = column[...]

time: 90.2 us -> 90.2 us (level)
  no operation moved by 1% of the time
where the time goes in v7:
time: 90.2 us; the launch traced here: 90.1 us
  Pallas kernels  89.5 us (99%)
    pallas_call x1, Pallas kernels, per_device(): pl.pallas_call(kernel, out_shape=outs, in_specs=[hbm, hbm, hbm], out_spec...  87.7 us

profile of v7, /device:TPU:35, one launch (start us, length us, event | category | flops | bytes accessed | tf_op | source)
XLA Modules:
  0.0 90.1 jit_solution(1892446367697250676)
XLA Ops:
  0.6 87.7 %shard_map.58 = (bf16[400,4096]{1,0:T(8,128)(2,1)S(1)}, f32[1,400]{1,0:T(1,128)S(1)}, bf16[16,4096]{1,0:T(8,128)(2,1)S(1)}) custom-call(f32[1,6400,256]{2,1,0:T(8,128)} %master_hbm.1, f32[1,256]{1,0:T(1,128)} %bitcast.4, f32[1,256]{1,0:T(1,128)} %bitcast.5), custom_call_target="tpu_custom_call" | custom-call | tf_op jit(solution)/shard_map/pallas_call | solution.py:257
  88.4 1.8 %shard_map.59 = (bf16[400,4096]{1,0:T(8,128)(2,1)}, f32[1,400]{1,0:T(1,128)}, bf16[16,4096]{1,0:T(8,128)(2,1)}) custom-call(bf16[400,4096]{1,0:T(8,128)(2,1)S(1)} %get-tuple-element.9.a, f32[1,400]{1,0:T(1,128)S(1)} %get-tuple-element.10.b, bf16[16,4096]{1,0:T(8,128)(2,1)S(1)} %get-tuple-element.11.c), custom_call_target="tpu_custom_call" | custom-call | tf_op jit(solution)/shard_map/pallas_call | solution.py:293

commit v8 on v6

--- a/solution.py
+++ b/solution.py
@@ -134,7 +134,7 @@
     totals[pair_of(me)] = total / WIDTH
     total_copies = [
         send(
-            totals.at[pair_of(me)], totals.at[pair_of(me)], total_s.at[0], total_r.at[i], owner, rows_of[len(FAR) + i]
+            totals.at[pair_of(me)], totals.at[pair_of(me)], total_s.at[0], total_r.at[0], owner, rows_of[len(FAR) + i]
         )
         for i in range(len(NEAR))
     ]
@@ -160,9 +160,9 @@
         )
 
     across_copies = [send_across(0, RAW, FIRST)]
+    settle(totals.at[pl.ds(0, len(NEAR))], total_r.at[0])
     land_copies = []
     for j, (_, dx, dc) in enumerate(NEAR):
-        total_copies[BACK[j]].wait_recv()
         device = peer_row(me, (1, dx, dc))
         scale_tile(device, 0, ROWS)
         land_copies.append(send(narrow.at[tile_at(device), :], landed.at[j], land_s.at[0], land_r.at[j], owner, across))
@@ -275,7 +275,7 @@
             dma((HALF,)),
             dma((2,)),
             dma((1,)), dma((1,)),
-            dma((1,)), dma((near,)),
+            dma((1,)), dma((1,)),
             dma((1,)), dma((1,)),
             dma((1,)), dma((near,)),
             dma((1,)), dma((1,)),

time: 90.2 us -> 91.2 us (1.011); the launches traced: 90.1 us -> 90.1 us
  no operation moved by 1% of the time
where the time goes in v8:
time: 91.2 us; the launch traced here: 90.1 us
  Pallas kernels  89.5 us (98%)
    pallas_call x1, Pallas kernels, per_device(): pl.pallas_call(kernel, out_shape=outs, in_specs=[hbm, hbm, hbm], out_spec...  87.7 us

profile of v8, /device:TPU:35, one launch (start us, length us, event | category | flops | bytes accessed | tf_op | source)
XLA Modules:
  0.0 90.1 jit_solution(2822005291036253387)
XLA Ops:
  0.6 87.7 %shard_map.58 = (bf16[400,4096]{1,0:T(8,128)(2,1)S(1)}, f32[1,400]{1,0:T(1,128)S(1)}, bf16[16,4096]{1,0:T(8,128)(2,1)S(1)}) custom-call(f32[1,6400,256]{2,1,0:T(8,128)} %master_hbm.1, f32[1,256]{1,0:T(1,128)} %bitcast.4, f32[1,256]{1,0:T(1,128)} %bitcast.5), custom_call_target="tpu_custom_call" | custom-call | tf_op jit(solution)/shard_map/pallas_call | solution.py:257
  88.3 1.8 %shard_map.59 = (bf16[400,4096]{1,0:T(8,128)(2,1)}, f32[1,400]{1,0:T(1,128)}, bf16[16,4096]{1,0:T(8,128)(2,1)}) custom-call(bf16[400,4096]{1,0:T(8,128)(2,1)S(1)} %get-tuple-element.9.a, f32[1,400]{1,0:T(1,128)S(1)} %get-tuple-element.10.b, bf16[16,4096]{1,0:T(8,128)(2,1)S(1)} %get-tuple-element.11.c), custom_call_target="tpu_custom_call" | custom-call | tf_op jit(solution)/shard_map/pallas_call | solution.py:293
